TPU v7x, 32 devices: a 4x4x1 block of a 4x4x8 slice. The times are simulated.
32 devices in a mesh: dp: 2 (over z, core), tp: 16 (over x, y).
Axes of the slice: x: 4, y: 4, z: 1, core: 2. Of those that a mesh axis runs over, the one named last changes fastest.
The devices are a block of a 4x4x8 slice.
Arguments:
- x: bfloat16 [4096, 2048], P('dp'), parts along dimension 0
- w_gate: bfloat16 [2048, 16384], P(None, 'tp')
- w_up: bfloat16 [2048, 16384], P(None, 'tp')
- w_down: bfloat16 [16384, 2048], P('tp')
Outputs:
- output: bfloat16 [4096, 2048], P('dp'), parts along dimension 0
There are 2 independent parts. A program takes and returns all parts, laid end to end along the dimension named above; an argument that names none is the same for every part.
All inputs are finite; a program needn't handle non-finite values.
Results may differ from a plain program's by a relative error of at most 0.016.
Values are sent between devices in bfloat16 or wider.
A program may use at most 768 MiB of HBM per device.

v0:
```python
import jax
import jax.numpy as jnp
from jax import lax
from jax.sharding import PartitionSpec as P


def solution(mesh):
    def step(x, w_gate, w_up, w_down):
        gate = jnp.dot(x, w_gate, preferred_element_type=jnp.float32)
        up = jnp.dot(x, w_up, preferred_element_type=jnp.float32)
        hidden = (jax.nn.gelu(gate) * up).astype(jnp.bfloat16)
        term = jnp.dot(hidden, w_down, preferred_element_type=jnp.float32).astype(jnp.bfloat16)
        return lax.psum(term, "tp")

    return jax.shard_map(
        step,
        mesh=mesh,
        in_specs=(P("dp", None), P(None, "tp"), P(None, "tp"), P("tp", None)),
        out_specs=P("dp", None),
        check_vma=False,
    )
```

profile of v0, /device:TPU:96, one launch (start us, length us, event | category | flops | bytes accessed | tf_op | source)
XLA Modules:
  0.0 196.5 jit_solution(3103049008991033589)
XLA Ops:
  6.5 0.0 all-reduce.2.cloned.1.call-start
  6.6 14.5 %fusion.17 = f32[2048,1024]{1,0:T(8,128)} fusion(bf16[2048,2048]{1,0:T(8,128)(2,1)} %param.4, bf16[2048,1024]{1,0:T(8,128)(2,1)} %param.5), kind=kOutput, calls=%fused_computation.19 | convolution fusion | flops 8589934592 | bytes 20971520 | tf_op jit(solution)/shard_map/dot_general | solution.py:9
  21.0 26.6 %convolution_convert_fusion = bf16[2048,2048]{1,0:T(8,128)(2,1)} fusion(bf16[1024,2048]{1,0:T(8,128)(2,1)} %param.7, f32[2048,1024]{1,0:T(8,128)} %fusion.17, bf16[2048,2048]{1,0:T(8,128)(2,1)} %param.4, bf16[2048,1024]{1,0:T(8,128)(2,1)} %param.6), kind=kOutput, calls=%fused_computation.10 | convolution fusion | flops 17205035008 | bytes 33554432 | tf_op jit(solution)/shard_map/dot_general | solution.py:12
  47.6 0.1 all-reduce.2.cloned.1.call-update
  47.7 133.5 %all-reduce.2.cloned.1.call-done = bf16[2048,2048]{1,0:T(8,128)(2,1)} async-done(((bf16[2048,2048]{1,0:T(8,128)(2,1)}), bf16[2048,2048]{1,0:T(8,128)(2,1)}) %all-reduce.2.cloned.1.call-update) | async-done | bytes 8388624 | tf_op jit(solution)/shard_map/psum | solution.py:13
  181.2 8.4 %copy.6 = bf16[2048,2048]{1,0:T(8,128)(2,1)} copy(bf16[2048,2048]{1,0:T(8,128)(2,1)} %all-reduce.2.cloned.1.call-done) | data formatting | bytes 16777216
Async XLA Ops:
  6.5 174.7 %all-reduce.2.cloned.1.call-start = ((), (), s32[]{:S(2)}) async-start(), calls=%async_computation | async-start | bytes 16777216 | tf_op jit(solution)/shard_map/psum | solution.py:13
Sparse Core Ops, SparseCore 0:
  47.8 133.3 all-reduce.1
where the time goes:
time: 197 us
  waiting for transfers between devices  134 us (68%)
  matrix products  41.1 us (21%)
  between operations  13.4 us (7%)
  local copies, waits for them, and re-layouts  8.44 us (4%)
    psum x1, waiting for transfers between devices, step(): return lax.psum(term, 'tp')  134 us
    dot_general x1, matrix products, step(): jnp.dot(hidden, w_down, preferred_element_type=jnp.float32)  26.6 us
    dot_general x1, matrix products, step(): gate = jnp.dot(x, w_gate, preferred_element_type=jnp.float32)  14.5 us
    unnamed x1, local copies, waits for them, and re-layouts  8.44 us
  transfers between devices with their start and end apart: 1, of which 1 were waited for; matrix products, arithmetic and copies ran while one was open for 0% of the time, Pallas kernels for 0%

commit v1 on v0

v1 whole, which is shorter than its diff:
```python
import functools
import math

import jax
import jax.numpy as jnp
from jax import lax
from jax.experimental import pallas as pl
from jax.experimental.pallas import tpu as pltpu
from jax.sharding import PartitionSpec as P

MESH = pl.DeviceIdType.MESH
BLOCK = 256
HID = 256
OUT = 512


def kernel(side, x_hbm, wg_hbm, wu_hbm, wd_hbm, y, xb, wg, wu, wd, hid, term, own,
           s1s, s1r, s2s, s2r, s3s, s3r, s4s, s4r, x_sem, wg_sem, wu_sem, wd_sem,
           send_sem, recv_sem):
    rows, d = x_hbm.shape
    f = wg.shape[1]
    blocks = rows // BLOCK
    sec = BLOCK // side
    piece = sec // side
    half = d // 2
    quarter = half // 2
    slots = term.shape[0]
    f32, bf16 = jnp.float32, jnp.bfloat16

    me = lax.axis_index("tp")
    i, j = me // side, me % side

    def up1(v):
        return lax.rem(v + 1, side)

    def dn1(v):
        return lax.rem(v + side - 1, side)

    along_x = (up1(i) * side + j, dn1(i) * side + j)
    along_y = (i * side + up1(j), i * side + dn1(j))
    first = (along_x, along_y)
    second = (along_y, along_x)
    pos = ((i, j), (j, i))

    barrier = pltpu.get_barrier_semaphore()
    for n in along_x + along_y:
        pl.semaphore_signal(barrier, inc=1, device_id={"tp": n}, device_id_type=MESH)

    def x_copy(b):
        return pltpu.make_async_copy(
            x_hbm.at[pl.ds(pl.multiple_of(b * BLOCK, BLOCK), BLOCK)],
            xb.at[lax.rem(b, 2)], x_sem.at[lax.rem(b, 2)])

    def g_copy(n):
        return pltpu.make_async_copy(
            wg_hbm.at[:, pl.ds(n * HID, HID)], wg.at[:, pl.ds(n * HID, HID)], wg_sem.at[n])

    def u_copy(n):
        return pltpu.make_async_copy(
            wu_hbm.at[:, pl.ds(n * HID, HID)], wu.at[:, pl.ds(n * HID, HID)], wu_sem.at[n])

    def d_copy(n):
        return pltpu.make_async_copy(
            wd_hbm.at[:, pl.ds(n * OUT, OUT)], wd.at[:, pl.ds(n * OUT, OUT)], wd_sem.at[n])

    x_copy(0).start()
    for n in range(f // HID):
        g_copy(n).start()
        u_copy(n).start()
    for n in range(d // OUT):
        d_copy(n).start()

    def remote(src, dst, stage, b, t, way, to):
        return pltpu.make_async_remote_copy(
            src_ref=src, dst_ref=dst, send_sem=send_sem.at[stage, b, t, way],
            recv_sem=recv_sem.at[stage, b, t, way], device_id={"tp": to}, device_id_type=MESH)

    def ds(start, size):
        return pl.ds(pl.multiple_of(start, size), size)

    def compute(b):
        slot = lax.rem(b, slots)
        xs = lax.rem(b, 2)
        x_copy(b).wait()

        @pl.when(b + 1 < blocks)
        def _():
            x_copy(b + 1).start()

        for n in range(f // HID):
            cols = pl.ds(n * HID, HID)

            @pl.when(b == 0)
            def _():
                g_copy(n).wait()
                u_copy(n).wait()

            gate = jnp.dot(xb[xs], wg[:, cols], preferred_element_type=f32)
            up = jnp.dot(xb[xs], wu[:, cols], preferred_element_type=f32)
            hid[:, cols] = (jax.nn.gelu(gate) * up).astype(bf16)
        for n in range(d // OUT):
            cols = pl.ds(n * OUT, OUT)

            @pl.when(b == 0)
            def _():
                d_copy(n).wait()

            term[slot, :, cols] = jnp.dot(hid[...], wd[:, cols], preferred_element_type=f32)

    def copies(stage, b, t):
        p, q = pos[t]
        cols = pl.ds(t * half, half)
        lo, hi = pl.ds(t * half, quarter), pl.ds(t * half + quarter, quarter)
        base = b * BLOCK
        if stage == 0:
            up, dn = first[t]
            h = sec // 2
            return (remote(s1s.at[b, t, pl.ds(0, h)], s1r.at[b, t, 0], 0, b, t, 0, up),
                    remote(s1s.at[b, t, pl.ds(h, h)], s1r.at[b, t, 1], 0, b, t, 1, dn))
        if stage == 1:
            up, dn = first[t]
            return (remote(s2s.at[b, t, 0], s2r.at[b, t, 0], 1, b, t, 0, up),
                    remote(s2s.at[b, t, 1], s2r.at[b, t, 1], 1, b, t, 1, dn))
        if stage == 2:
            up, dn = second[t]
            return (remote(s3s.at[b, t, :, pl.ds(0, quarter)], s3r.at[b, t, 0], 2, b, t, 0, up),
                    remote(s3s.at[b, t, :, pl.ds(quarter, quarter)], s3r.at[b, t, 1], 2, b, t, 1, dn))
        if stage == 3:
            up, dn = second[t]
            return (remote(s4s.at[b, t, 0], s4r.at[b, t, 0], 3, b, t, 0, up),
                    remote(s4s.at[b, t, 1], s4r.at[b, t, 1], 3, b, t, 1, dn))
        if stage == 4:
            up, dn = second[t]
            at = y.at[ds(base + p * sec + q * piece, piece), cols]
            return remote(at, at, 4, b, t, 0, up), remote(at, at, 4, b, t, 1, dn)
        if stage == 5:
            up, dn = second[t]
            a0 = y.at[ds(base + p * sec + dn1(q) * piece, piece), lo]
            a1 = y.at[ds(base + p * sec + up1(q) * piece, piece), hi]
            return remote(a0, a0, 5, b, t, 0, up), remote(a1, a1, 5, b, t, 1, dn)
        if stage == 6:
            up, dn = first[t]
            at = y.at[ds(base + p * sec, sec), cols]
            return remote(at, at, 6, b, t, 0, up), remote(at, at, 6, b, t, 1, dn)
        up, dn = first[t]
        h = sec // 2
        a0 = y.at[ds(base + dn1(p) * sec, h), cols]
        a1 = y.at[ds(base + up1(p) * sec + h, h), cols]
        return remote(a0, a0, 7, b, t, 0, up), remote(a1, a1, 7, b, t, 1, dn)

    def arrivals(stage, b, t):
        p, q = pos[t]
        cols = pl.ds(t * half, half)
        lo, hi = pl.ds(t * half, quarter), pl.ds(t * half + quarter, quarter)
        base = b * BLOCK
        opp = lambda v: lax.rem(v + 2, side)
        if stage < 4:
            r = (s1r, s2r, s3r, s4r)[stage]
            at = (r.at[b, t, 0], r.at[b, t, 1])
        elif stage == 4:
            at = (y.at[ds(base + p * sec + dn1(q) * piece, piece), cols],
                  y.at[ds(base + p * sec + up1(q) * piece, piece), cols])
        elif stage == 5:
            row = ds(base + p * sec + opp(q) * piece, piece)
            at = (y.at[row, lo], y.at[row, hi])
        elif stage == 6:
            at = (y.at[ds(base + dn1(p) * sec, sec), cols],
                  y.at[ds(base + up1(p) * sec, sec), cols])
        else:
            h = sec // 2
            at = (y.at[ds(base + opp(p) * sec, h), cols],
                  y.at[ds(base + opp(p) * sec + h, h), cols])
        return tuple(remote(a, a, stage, b, t, way, me) for way, a in enumerate(at))

    def start(stage, b, t):
        for c in copies(stage, b, t):
            c.start()

    def arrive(stage, b, t):
        for c in arrivals(stage, b, t):
            c.wait_recv()

    def stage0(b):
        slot = lax.rem(b, slots)
        for t in range(2):
            p, _ = pos[t]
            rows_ = ds(lax.rem(p + 2, side) * sec, sec)
            s1s[b, t] = term[slot, rows_, pl.ds(t * half, half)].astype(bf16)
            start(0, b, t)

    def stage1(b):
        slot = lax.rem(b, slots)
        h = sec // 2
        for t in range(2):
            p, _ = pos[t]
            cols = pl.ds(t * half, half)
            arrive(0, b, t)
            r, l = up1(p) * sec, dn1(p) * sec
            s2s[b, t, 0, pl.ds(0, h)] = (
                term[slot, ds(r, h), cols] + s1r[b, t, 0].astype(f32)).astype(bf16)
            s2s[b, t, 0, pl.ds(h, h)] = term[slot, ds(r + h, h), cols].astype(bf16)
            s2s[b, t, 1, pl.ds(0, h)] = term[slot, ds(l, h), cols].astype(bf16)
            s2s[b, t, 1, pl.ds(h, h)] = (
                term[slot, ds(l + h, h), cols] + s1r[b, t, 1].astype(f32)).astype(bf16)
            start(1, b, t)

    def stage2(b):
        slot = lax.rem(b, slots)
        for t in range(2):
            p, q = pos[t]
            cols = pl.ds(t * half, half)
            arrive(1, b, t)
            own[b, t] = (term[slot, ds(p * sec, sec), cols]
                         + s2r[b, t, 0].astype(f32) + s2r[b, t, 1].astype(f32))
            s3s[b, t] = own[b, t, ds(lax.rem(q + 2, side) * piece, piece), :].astype(bf16)
            start(2, b, t)

    def stage3(b):
        lo, hi = pl.ds(0, quarter), pl.ds(quarter, quarter)
        for t in range(2):
            _, q = pos[t]
            arrive(2, b, t)
            r, l = ds(up1(q) * piece, piece), ds(dn1(q) * piece, piece)
            s4s[b, t, 0, :, lo] = (own[b, t, r, lo] + s3r[b, t, 0].astype(f32)).astype(bf16)
            s4s[b, t, 0, :, hi] = own[b, t, r, hi].astype(bf16)
            s4s[b, t, 1, :, lo] = own[b, t, l, lo].astype(bf16)
            s4s[b, t, 1, :, hi] = (own[b, t, l, hi] + s3r[b, t, 1].astype(f32)).astype(bf16)
            start(3, b, t)

    def stage4(b):
        for t in range(2):
            p, q = pos[t]
            arrive(3, b, t)
            y[ds(b * BLOCK + p * sec + q * piece, piece), pl.ds(t * half, half)] = (
                own[b, t, ds(q * piece, piece), :]
                + s4r[b, t, 0].astype(f32) + s4r[b, t, 1].astype(f32)).astype(bf16)
            start(4, b, t)

    def pass_on(stage):
        def run(b):
            for t in range(2):
                arrive(stage - 1, b, t)
                start(stage, b, t)
        return run

    def finish(b):
        for t in range(2):
            arrive(7, b, t)

    stages = [stage0, stage1, stage2, stage3, stage4, pass_on(5), pass_on(6), pass_on(7), finish]

    def step(n, _):
        @pl.when(n < blocks)
        def _():
            compute(n)

        @pl.when(n == 0)
        def _():
            pl.semaphore_wait(barrier, 4)

        for k, stage in enumerate(stages):
            @pl.when((n >= k) & (n < blocks + k))
            def _():
                stage(n - k)
        return 0

    lax.fori_loop(0, blocks + len(stages) - 1, step, 0)

    def drain(b, _):
        for stage in range(8):
            for t in range(2):
                for c in copies(stage, b, t):
                    c.wait_send()
        return 0

    lax.fori_loop(0, blocks, drain, 0)


def solution(mesh):
    side = math.isqrt(mesh.shape["tp"])

    def step(x, w_gate, w_up, w_down):
        rows, d = x.shape
        f = w_gate.shape[1]
        blocks, sec = rows // BLOCK, BLOCK // side
        piece, half = sec // side, d // 2
        bf16, f32 = jnp.bfloat16, jnp.float32
        return pl.pallas_call(
            functools.partial(kernel, side),
            out_shape=jax.ShapeDtypeStruct((rows, d), bf16),
            in_specs=[pl.BlockSpec(memory_space=pl.ANY)] * 4,
            out_specs=pl.BlockSpec(memory_space=pltpu.VMEM),
            scratch_shapes=[
                pltpu.VMEM((2, BLOCK, d), bf16),
                pltpu.VMEM((d, f), bf16),
                pltpu.VMEM((d, f), bf16),
                pltpu.VMEM((f, d), bf16),
                pltpu.VMEM((BLOCK, f), bf16),
                pltpu.VMEM((3, BLOCK, d), f32),
                pltpu.VMEM((blocks, 2, sec, half), f32),
                pltpu.VMEM((blocks, 2, sec, half), bf16),
                pltpu.VMEM((blocks, 2, 2, sec // 2, half), bf16),
                pltpu.VMEM((blocks, 2, 2, sec, half), bf16),
                pltpu.VMEM((blocks, 2, 2, sec, half), bf16),
                pltpu.VMEM((blocks, 2, piece, half), bf16),
                pltpu.VMEM((blocks, 2, 2, piece, half // 2), bf16),
                pltpu.VMEM((blocks, 2, 2, piece, half), bf16),
                pltpu.VMEM((blocks, 2, 2, piece, half), bf16),
                pltpu.SemaphoreType.DMA((2,)),
                pltpu.SemaphoreType.DMA((f // HID,)),
                pltpu.SemaphoreType.DMA((f // HID,)),
                pltpu.SemaphoreType.DMA((d // OUT,)),
                pltpu.SemaphoreType.DMA((8, blocks, 2, 2)),
                pltpu.SemaphoreType.DMA((8, blocks, 2, 2)),
            ],
            compiler_params=pltpu.CompilerParams(
                collective_id=0, has_side_effects=True, vmem_limit_bytes=60 * 2**20),
        )(x, w_gate, w_up, w_down)

    return jax.shard_map(
        step,
        mesh=mesh,
        in_specs=(P("dp", None), P(None, "tp"), P(None, "tp"), P("tp", None)),
        out_specs=P("dp", None),
        check_vma=False,
    )
```

time: 197 us -> 124 us (0.63)
  waiting for transfers between devices: 134 us -> 0 us
  Pallas kernels: 0 us -> 116 us
  matrix products: 41.1 us -> 0 us
  between operations: 13.4 us -> 0.01 us
    psum x1 -> x0, waiting for transfers between devices: 134 us -> none  [step(): return lax.psum(term, 'tp')]
    pallas_call x0 -> x1, Pallas kernels: none -> 116 us  [step(): pl.pallas_call(functools.partial(kernel, side), out_shape=jax.ShapeDtypeS...]
    dot_general x2 -> x0, matrix products: 41.1 us -> none  [the longest x1 26.6 us: step(): jnp.dot(hidden, w_down, preferred_element_type=jnp.float32)]
  transfers between devices with their start and end apart: 1 -> 0, of which waited for: 1 -> 0; matrix products, arithmetic and copies ran while one was open for 0% -> 0% of each run, Pallas kernels for 0% -> 0%
where the time goes in v1:
time: 124 us
  Pallas kernels  116 us (94%)
  local copies, waits for them, and re-layouts  8.44 us (7%)
    pallas_call x1, Pallas kernels, step(): pl.pallas_call(functools.partial(kernel, side), out_shape=jax.ShapeDtypeS...  116 us
    unnamed x1, local copies, waits for them, and re-layouts  8.44 us

profile of v1, /device:TPU:96, one launch (start us, length us, event | category | flops | bytes accessed | tf_op | source)
XLA Modules:
  0.0 124.2 jit_solution(738780014432790800)
XLA Ops:
  0.0 115.8 %shard_map.46 = bf16[2048,2048]{1,0:T(8,128)(2,1)} custom-call(bf16[2048,2048]{1,0:T(8,128)(2,1)} %x_hbm.1, bf16[2048,1024]{1,0:T(8,128)(2,1)} %wg_hbm.1, bf16[2048,1024]{1,0:T(8,128)(2,1)} %wu_hbm.1, bf16[1024,2048]{1,0:T(8,128)(2,1)} %wd_hbm.1), custom_call_target="tpu_custom_call" | custom-call | tf_op jit(solution)/shard_map/pallas_call | solution.py:288
  115.8 8.4 %copy.6 = bf16[2048,2048]{1,0:T(8,128)(2,1)} copy(bf16[2048,2048]{1,0:T(8,128)(2,1)} %shard_map.46) | data formatting | bytes 16777216

commit v2 on v0

v2 whole, which is shorter than its diff:
```python
import functools
import math

import jax
import jax.numpy as jnp
from jax import lax
from jax.experimental import pallas as pl
from jax.experimental.pallas import tpu as pltpu
from jax.sharding import PartitionSpec as P

MESH = pl.DeviceIdType.MESH
BLOCK = 256
HID0, OUT0 = 256, 512
HID, OUT = 512, 1024
SPLIT = 5


def kernel(side, x_hbm, wg_hbm, wu_hbm, wd_hbm, y, xb, wg, wu, wd, hid, term, own,
           s1s, s1r, s2s, s2r, s3s, s3r, s4s, s4r, x_sem, wg_sem, wu_sem, wd_sem,
           send_sem, recv_sem):
    rows, d = x_hbm.shape
    f = wg.shape[1]
    blocks = rows // BLOCK
    pairs = blocks // 2
    sec = BLOCK // side
    piece = sec // side
    h = sec // 2
    half = d // 2
    quarter = half // 2
    slots = term.shape[0]
    f32, bf16 = jnp.float32, jnp.bfloat16

    me = lax.axis_index("tp")
    i, j = me // side, me % side

    def up1(v):
        return lax.rem(v + 1, side)

    def dn1(v):
        return lax.rem(v + side - 1, side)

    def opp(v):
        return lax.rem(v + 2, side)

    along_x = (up1(i) * side + j, dn1(i) * side + j)
    along_y = (i * side + up1(j), i * side + dn1(j))
    first = (along_x, along_y)
    second = (along_y, along_x)
    pos = ((i, j), (j, i))

    barrier = pltpu.get_barrier_semaphore()
    for n in along_x + along_y:
        pl.semaphore_signal(barrier, inc=1, device_id={"tp": n}, device_id_type=MESH)

    def ds(start, size):
        return pl.ds(pl.multiple_of(start, size), size)

    def x_copy(b):
        return pltpu.make_async_copy(
            x_hbm.at[ds(b * BLOCK, BLOCK)], xb.at[lax.rem(b, 2)], x_sem.at[lax.rem(b, 2)])

    pieces0 = [(0, HID0), (HID0, HID0), (2 * HID0, f - 2 * HID0)]

    def load(src, dst, sem, n, first_col, size):
        cols = pl.ds(first_col, size)
        return pltpu.make_async_copy(src.at[:, cols], dst.at[:, cols], sem.at[n])

    def load_in(n):
        return load(wg_hbm, wg, wg_sem, n, *pieces0[n]), load(wu_hbm, wu, wu_sem, n, *pieces0[n])

    def load_out(n):
        return load(wd_hbm, wd, wd_sem, n, n * OUT0, OUT0)

    x_copy(0).start()
    for n in range(3):
        for c in load_in(n):
            c.start()

    def hidden(xs, first_col, size):
        cols = pl.ds(first_col, size)
        gate = jnp.dot(xb[xs], wg[:, cols], preferred_element_type=f32)
        up = jnp.dot(xb[xs], wu[:, cols], preferred_element_type=f32)
        hid[:, cols] = (jax.nn.gelu(gate) * up).astype(bf16)

    def down(slot, n, size):
        cols = pl.ds(n * size, size)
        term[slot, :, cols] = jnp.dot(hid[...], wd[:, cols], preferred_element_type=f32)

    def compute1(b):
        x_copy(b).wait()
        for n in range(f // HID):
            hidden(lax.rem(b, 2), n * HID, HID)

    def compute2(b):
        for n in range(d // OUT):
            down(lax.rem(b, slots), n, OUT)

        @pl.when(b + 2 < blocks)
        def _():
            x_copy(b + 2).start()

    def compute(b):
        compute1(b)
        compute2(b)

    def cols_of(t):
        return pl.ds(t * half, half)

    def two(g):
        return pl.ds(2 * g, 2)

    def far(b, t):
        return [(s1s.at[t, b, pl.ds(w * h, h)], s1r.at[t, w, b], first[t][w]) for w in range(2)]

    def near(b, t):
        return [(s2s.at[t, w, b], s2r.at[t, w, b], first[t][w]) for w in range(2)]

    def near_part(b, t, own_half):
        k = [pl.ds((1 - w if own_half else w) * h, h) for w in range(2)]
        return [(s2s.at[t, w, b, k[w]], s2r.at[t, w, b, k[w]], first[t][w]) for w in range(2)]

    def far2(g, t):
        return [(s3s.at[t, two(g), :, pl.ds(w * quarter, quarter)], s3r.at[t, w, two(g)],
                 second[t][w]) for w in range(2)]

    def near2(g, t):
        return [(s4s.at[t, w, two(g)], s4r.at[t, w, two(g)], second[t][w]) for w in range(2)]

    def gather1(g, t):
        p, q = pos[t]
        at = y.at[two(g), ds(p * sec + q * piece, piece), cols_of(t)]
        return [(at, at, second[t][w]) for w in range(2)]

    def gather2(g, t):
        p, q = pos[t]
        at = [y.at[two(g), ds(p * sec + v * piece, piece), pl.ds(t * half + w * quarter, quarter)]
              for w, v in enumerate((dn1(q), up1(q)))]
        return [(at[w], at[w], second[t][w]) for w in range(2)]

    def gather3(bs, t):
        p, _ = pos[t]
        at = y.at[bs, ds(p * sec, sec), cols_of(t)]
        return [(at, at, first[t][w]) for w in range(2)]

    def gather4(bs, t):
        p, _ = pos[t]
        at = [y.at[bs, ds(v * sec + w * h, h), cols_of(t)] for w, v in enumerate((dn1(p), up1(p)))]
        return [(at[w], at[w], first[t][w]) for w in range(2)]

    FAR, NEAR, FAR2, NEAR2, G1, G2, G3, G4 = range(8)
    own_sem = 8 * blocks

    def start(copies, kind, sem):
        for src, dst, to in copies:
            pltpu.make_async_remote_copy(
                src_ref=src, dst_ref=dst, send_sem=send_sem.at[kind], recv_sem=recv_sem.at[sem],
                device_id={"tp": to}, device_id_type=MESH).start()

    def arrive(like, sem):
        pltpu.make_async_copy(like, like, recv_sem.at[sem]).wait()

    def base_of(kind):
        return kind * blocks

    def pack(b, t, split):
        slot = lax.rem(b, slots)
        p, _ = pos[t]
        c = cols_of(t)
        s1s[t, b] = term[slot, ds(opp(p) * sec, sec), c].astype(bf16)
        start(far(b, t), FAR, base_of(FAR) + b)
        s2s[t, 0, b, pl.ds(h, h)] = term[slot, ds(up1(p) * sec + h, h), c].astype(bf16)
        s2s[t, 1, b, pl.ds(0, h)] = term[slot, ds(dn1(p) * sec, h), c].astype(bf16)
        if split:
            start(near_part(b, t, True), NEAR, own_sem + b)

    def reduce1(b, split):
        slot = lax.rem(b, slots)
        arrive(s1r.at[:, :, b], base_of(FAR) + b)
        for t in range(2):
            p, _ = pos[t]
            c = cols_of(t)
            s2s[t, 0, b, pl.ds(0, h)] = (
                term[slot, ds(up1(p) * sec, h), c] + s1r[t, 0, b].astype(f32)).astype(bf16)
            s2s[t, 1, b, pl.ds(h, h)] = (
                term[slot, ds(dn1(p) * sec + h, h), c] + s1r[t, 1, b].astype(f32)).astype(bf16)
            start(near_part(b, t, False) if split else near(b, t), NEAR, base_of(NEAR) + b)

    def reduce2(g):
        for b in (2 * g, 2 * g + 1):
            if b < SPLIT:
                arrive(s1r.at[:, :, b], own_sem + b)
                arrive(s1r.at[:, :, b], base_of(NEAR) + b)
            else:
                arrive(s2r.at[:, :, b], base_of(NEAR) + b)
        for t in range(2):
            p, q = pos[t]
            for b in (2 * g, 2 * g + 1):
                own[t, b] = (term[b % slots, ds(p * sec, sec), cols_of(t)]
                             + s2r[t, 0, b].astype(f32) + s2r[t, 1, b].astype(f32))
                s3s[t, b] = own[t, b, ds(opp(q) * piece, piece), :].astype(bf16)
            start(far2(g, t), FAR2, base_of(FAR2) + g)

    def reduce3(g):
        lo, hi = pl.ds(0, quarter), pl.ds(quarter, quarter)
        arrive(s3r.at[:, :, two(g)], base_of(FAR2) + g)
        for t in range(2):
            _, q = pos[t]
            r, l = ds(up1(q) * piece, piece), ds(dn1(q) * piece, piece)
            for b in (2 * g, 2 * g + 1):
                s4s[t, 0, b, :, lo] = (own[t, b, r, lo] + s3r[t, 0, b].astype(f32)).astype(bf16)
                s4s[t, 0, b, :, hi] = own[t, b, r, hi].astype(bf16)
                s4s[t, 1, b, :, lo] = own[t, b, l, lo].astype(bf16)
                s4s[t, 1, b, :, hi] = (own[t, b, l, hi] + s3r[t, 1, b].astype(f32)).astype(bf16)
            start(near2(g, t), NEAR2, base_of(NEAR2) + g)

    def reduce4(g):
        arrive(s4r.at[:, :, two(g)], base_of(NEAR2) + g)
        for t in range(2):
            p, q = pos[t]
            for b in (2 * g, 2 * g + 1):
                y[b, ds(p * sec + q * piece, piece), cols_of(t)] = (
                    own[t, b, ds(q * piece, piece), :]
                    + s4r[t, 0, b].astype(f32) + s4r[t, 1, b].astype(f32)).astype(bf16)
            start(gather1(g, t), G1, base_of(G1) + g)

    def send2(g):
        arrive(s4r.at[:, :, two(g)], base_of(G1) + g)
        for t in range(2):
            start(gather2(g, t), G2, base_of(G2) + g)

    def units(g):
        return [(two(g), g)] if g < pairs - 1 else [(pl.ds(b, 1), b) for b in (2 * g, 2 * g + 1)]

    def send3(g):
        arrive(s3r.at[:, :, two(g)], base_of(G2) + g)
        for bs, u in units(g):
            for t in range(2):
                start(gather3(bs, t), G3, base_of(G3) + u)

    def send4(g, n=None):
        for k, (bs, u) in enumerate(units(g)):
            if n is None or n == k:
                arrive(s2r.at[:, :, bs], base_of(G3) + u)
                for t in range(2):
                    start(gather4(bs, t), G4, base_of(G4) + u)

    x_copy(0).wait()
    for n in range(3):
        for c in load_in(n):
            c.wait()
        if n == 1:
            for k in range(d // OUT0):
                load_out(k).start()
            x_copy(1).start()
        hidden(0, *pieces0[n])
    for t in range(2):
        for n in range(t * half // OUT0, (t + 1) * half // OUT0):
            load_out(n).wait()
            down(0, n, OUT0)
        if t == 0:
            pl.semaphore_wait(barrier, 4)
        pack(0, t, True)
    x_copy(2).start()

    compute1(1)
    reduce1(0, True)
    compute2(1)
    pack(1, 0, True)
    pack(1, 1, True)

    beside = {
        3: [(reduce2, 0)],
        4: [(reduce3, 0)],
        5: [(reduce2, 1), (reduce4, 0)],
        6: [(reduce3, 1), (send2, 0)],
        7: [(reduce2, 2), (reduce4, 1), (send3, 0)],
    }

    def step(b, _):
        compute(b)

        @pl.when(b < SPLIT)
        def _():
            pack(b, 0, True)
            pack(b, 1, True)

        @pl.when(b >= SPLIT)
        def _():
            pack(b, 0, False)
            pack(b, 1, False)

        @pl.when(b <= SPLIT)
        def _():
            reduce1(b - 1, True)

        @pl.when(b > SPLIT)
        def _():
            reduce1(b - 1, False)

        for k, tasks in beside.items():
            @pl.when(b == k)
            def _():
                for task, g in tasks:
                    task(g)
        return 0

    lax.fori_loop(2, blocks, step, 0)

    reduce1(blocks - 1, SPLIT == blocks)
    for task, *args in [
        (reduce3, 2), (send2, 1),
        (reduce2, 3), (reduce4, 2), (send3, 1),
        (reduce3, 3), (send2, 2), (send4, 0),
        (reduce4, 3), (send3, 2),
        (send2, 3), (send4, 1),
        (send3, 3), (send4, 2), (send4, 3, 0), (send4, 3, 1),
    ]:
        task(*args)
    for g in range(pairs):
        for bs, u in units(g):
            arrive(s1r.at[:, :, bs], base_of(G4) + u)

    for kind, like in enumerate((s1s, s2s, s3s, s4s, s4s, s3s, s2s, s1s)):
        pltpu.make_async_copy(like, like, send_sem.at[kind]).wait()


def solution(mesh):
    side = math.isqrt(mesh.shape["tp"])

    def step(x, w_gate, w_up, w_down):
        rows, d = x.shape
        f = w_gate.shape[1]
        blocks, sec = rows // BLOCK, BLOCK // side
        piece, half = sec // side, d // 2
        bf16, f32 = jnp.bfloat16, jnp.float32
        return pl.pallas_call(
            functools.partial(kernel, side),
            out_shape=pltpu.VMEM((blocks, BLOCK, d), bf16),
            in_specs=[pl.BlockSpec(memory_space=pl.ANY)] * 4,
            out_specs=pl.BlockSpec(memory_space=pltpu.VMEM),
            scratch_shapes=[
                pltpu.VMEM((2, BLOCK, d), bf16),
                pltpu.VMEM((d, f), bf16),
                pltpu.VMEM((d, f), bf16),
                pltpu.VMEM((f, d), bf16),
                pltpu.VMEM((BLOCK, f), bf16),
                pltpu.VMEM((4, BLOCK, d), f32),
                pltpu.VMEM((2, blocks, sec, half), f32),
                pltpu.VMEM((2, blocks, sec, half), bf16),
                pltpu.VMEM((2, 2, blocks, sec // 2, half), bf16),
                pltpu.VMEM((2, 2, blocks, sec, half), bf16),
                pltpu.VMEM((2, 2, blocks, sec, half), bf16),
                pltpu.VMEM((2, blocks, piece, half), bf16),
                pltpu.VMEM((2, 2, blocks, piece, half // 2), bf16),
                pltpu.VMEM((2, 2, blocks, piece, half), bf16),
                pltpu.VMEM((2, 2, blocks, piece, half), bf16),
                pltpu.SemaphoreType.DMA((2,)),
                pltpu.SemaphoreType.DMA((3,)),
                pltpu.SemaphoreType.DMA((3,)),
                pltpu.SemaphoreType.DMA((d // OUT0,)),
                pltpu.SemaphoreType.DMA((8,)),
                pltpu.SemaphoreType.DMA((8 * blocks + SPLIT,)),
            ],
            compiler_params=pltpu.CompilerParams(
                collective_id=0, has_side_effects=True, vmem_limit_bytes=50 * 2**20),
        )(x, w_gate, w_up, w_down).reshape(rows, d)

    return jax.shard_map(
        step,
        mesh=mesh,
        in_specs=(P("dp", None), P(None, "tp"), P(None, "tp"), P("tp", None)),
        out_specs=P("dp", None),
        check_vma=False,
    )
```

time: 197 us -> 105 us (0.53)
  waiting for transfers between devices: 134 us -> 0 us
  Pallas kernels: 0 us -> 101 us
  matrix products: 41.1 us -> 0 us
  between operations: 13.4 us -> 0.01 us
  local copies, waits for them, and re-layouts: 8.44 us -> 3.4 us
    psum x1 -> x0, waiting for transfers between devices: 134 us -> none  [step(): return lax.psum(term, 'tp')]
    pallas_call x0 -> x1, Pallas kernels: none -> 101 us  [step(): pl.pallas_call(functools.partial(kernel, side), out_shape=pltpu.VMEM((blo...]
    dot_general x2 -> x0, matrix products: 41.1 us -> none  [the longest x1 26.6 us: step(): jnp.dot(hidden, w_down, preferred_element_type=jnp.float32)]
    unnamed x1, local copies, waits for them, and re-layouts: 8.44 us -> 3.4 us
  transfers between devices with their start and end apart: 1 -> 0, of which waited for: 1 -> 0; matrix products, arithmetic and copies ran while one was open for 0% -> 0% of each run, Pallas kernels for 0% -> 0%
where the time goes in v2:
time: 105 us; the launch traced here: 104 us
  Pallas kernels  101 us (96%)
  local copies, waits for them, and re-layouts  3.4 us (3%)
    pallas_call x1, Pallas kernels, step(): pl.pallas_call(functools.partial(kernel, side), out_shape=pltpu.VMEM((blo...  101 us
    unnamed x1, local copies, waits for them, and re-layouts  3.4 us

profile of v2, /device:TPU:96, one launch (start us, length us, event | category | flops | bytes accessed | tf_op | source)
XLA Modules:
  0.0 104.5 jit_solution(5333458530966291644)
XLA Ops:
  0.0 101.1 %shard_map.46 = bf16[8,256,2048]{2,1,0:T(8,128)(2,1)S(1)} custom-call(bf16[2048,2048]{1,0:T(8,128)(2,1)} %x_hbm.1, bf16[2048,1024]{1,0:T(8,128)(2,1)} %wg_hbm.1, bf16[2048,1024]{1,0:T(8,128)(2,1)} %wu_hbm.1, bf16[1024,2048]{1,0:T(8,128)(2,1)} %wd_hbm.1), custom_call_target="tpu_custom_call" | custom-call | tf_op jit(solution)/shard_map/pallas_call | solution.py:336
  101.1 3.4 %copy.6 = bf16[2048,2048]{1,0:T(8,128)(2,1)} copy(bf16[2048,2048]{1,0:T(8,128)(2,1)S(1)} %bitcast.1) | data formatting | bytes 16777216

commit v3 on v2

v3 whole, which is shorter than its diff:
```python
import functools
import math

import jax
import jax.numpy as jnp
from jax import lax
from jax.experimental import pallas as pl
from jax.experimental.pallas import tpu as pltpu
from jax.sharding import PartitionSpec as P

MESH = pl.DeviceIdType.MESH
BLOCK = 256
HID0, OUT0 = 256, 1024
HID, OUT = 512, 1024
GROUPS = 4
SPLIT = 5


def kernel(side, x_hbm, wg_hbm, wu_hbm, wd_hbm, y, xb, wg, wu, wd, hid, term, own,
           s1s, s1r, s2s, s2r, s3s, s3r, s4s, s4r, x_sem, wg_sem, wu_sem, wd_sem,
           send_sem, recv_sem):
    rows, d = x_hbm.shape
    f = wg.shape[1]
    blocks = rows // BLOCK
    sec = BLOCK // side
    piece = sec // side
    h = sec // 2
    half = d // 2
    quarter = half // 2
    slots = term.shape[0]
    f32, bf16 = jnp.float32, jnp.bfloat16

    me = lax.axis_index("tp")
    i, j = me // side, me % side

    def up1(v):
        return lax.rem(v + 1, side)

    def dn1(v):
        return lax.rem(v + side - 1, side)

    def opp(v):
        return lax.rem(v + 2, side)

    along_x = (up1(i) * side + j, dn1(i) * side + j)
    along_y = (i * side + up1(j), i * side + dn1(j))
    first = (along_x, along_y)
    second = (along_y, along_x)
    pos = ((i, j), (j, i))

    barrier = pltpu.get_barrier_semaphore()
    for n in along_x + along_y:
        pl.semaphore_signal(barrier, inc=1, device_id={"tp": n}, device_id_type=MESH)

    def ds(start, size):
        return pl.ds(pl.multiple_of(start, size), size)

    def x_copy(b):
        return pltpu.make_async_copy(
            x_hbm.at[ds(b * BLOCK, BLOCK)], xb.at[lax.rem(b, 2)], x_sem.at[lax.rem(b, 2)])

    pieces0 = [(0, HID0), (HID0, HID0), (2 * HID0, f - 2 * HID0)]

    def load(src, dst, sem, n, first_col, size):
        cols = pl.ds(first_col, size)
        return pltpu.make_async_copy(src.at[:, cols], dst.at[:, cols], sem.at[n])

    def load_in(n):
        return load(wg_hbm, wg, wg_sem, n, *pieces0[n]), load(wu_hbm, wu, wu_sem, n, *pieces0[n])

    def load_out(n):
        return load(wd_hbm, wd, wd_sem, n, n * OUT0, OUT0)

    x_copy(0).start()
    for n in range(3):
        for c in load_in(n):
            c.start()

    def hidden(xs, first_col, size):
        cols = pl.ds(first_col, size)
        gate = jnp.dot(xb[xs], wg[:, cols], preferred_element_type=f32)
        up = jnp.dot(xb[xs], wu[:, cols], preferred_element_type=f32)
        hid[:, cols] = (jax.nn.gelu(gate) * up).astype(bf16)

    def down(slot, n, size):
        cols = pl.ds(n * size, size)
        term[slot, :, cols] = jnp.dot(hid[...], wd[:, cols], preferred_element_type=f32)

    def compute1(b):
        x_copy(b).wait()
        for n in range(f // HID):
            hidden(lax.rem(b, 2), n * HID, HID)

    def compute2(b):
        for n in range(d // OUT):
            down(lax.rem(b, slots), n, OUT)

        @pl.when(b + 2 < blocks)
        def _():
            x_copy(b + 2).start()

    def compute(b):
        compute1(b)
        compute2(b)

    def far(lo, n, t):
        bs = pl.ds(lo, n)
        return [(s1s.at[t, bs, pl.ds(w * h, h)], s1r.at[t, w, bs], first[t][w]) for w in range(2)]

    def near(lo, n, t):
        bs = pl.ds(lo, n)
        return [(s2s.at[t, w, bs], s2r.at[t, w, bs], first[t][w]) for w in range(2)]

    def near_part(b, t, own_half):
        k = [pl.ds((1 - w if own_half else w) * h, h) for w in range(2)]
        return [(s2s.at[t, w, b, k[w]], s2r.at[t, w, b, k[w]], first[t][w]) for w in range(2)]

    def far2(lo, n, t):
        bs = pl.ds(lo, n)
        return [(s3s.at[t, bs, :, pl.ds(w * quarter, quarter)], s3r.at[t, w, bs], second[t][w])
                for w in range(2)]

    def near2(lo, n, t):
        bs = pl.ds(lo, n)
        return [(s4s.at[t, w, bs], s4r.at[t, w, bs], second[t][w]) for w in range(2)]

    def gather1(lo, n, t):
        p, q = pos[t]
        at = y.at[pl.ds(lo, n), ds(p * sec + q * piece, piece), pl.ds(t * half, half)]
        return [(at, at, second[t][w]) for w in range(2)]

    def gather2(lo, n, t):
        p, q = pos[t]
        at = [y.at[pl.ds(lo, n), ds(p * sec + v * piece, piece),
                   pl.ds(t * half + w * quarter, quarter)] for w, v in enumerate((dn1(q), up1(q)))]
        return [(at[w], at[w], second[t][w]) for w in range(2)]

    def gather3(lo, n, t):
        p, _ = pos[t]
        at = y.at[pl.ds(lo, n), ds(p * sec, sec), pl.ds(t * half, half)]
        return [(at, at, first[t][w]) for w in range(2)]

    def gather4(lo, n, t):
        p, _ = pos[t]
        at = [y.at[pl.ds(lo, n), ds(v * sec + w * h, h), pl.ds(t * half, half)]
              for w, v in enumerate((dn1(p), up1(p)))]
        return [(at[w], at[w], first[t][w]) for w in range(2)]

    FAR, NEAR, FAR2, NEAR2 = 0, blocks, 2 * blocks, 2 * blocks + GROUPS
    OWN = NEAR2 + GROUPS
    LAST = OWN + SPLIT
    S_FAR, S_NEAR, S_FAR2, S_NEAR2 = range(4)

    def start(copies, sent, sem):
        for src, dst, to in copies:
            pltpu.make_async_remote_copy(
                src_ref=src, dst_ref=dst, send_sem=send_sem.at[sent], recv_sem=recv_sem.at[sem],
                device_id={"tp": to}, device_id_type=MESH).start()

    def arrive(like, sem):
        pltpu.make_async_copy(like, like, recv_sem.at[sem]).wait()

    def pack(lo, n, split, streams=range(2)):
        for t in streams:
            p, _ = pos[t]
            c = pl.ds(t * half, half)
            for k in range(n):
                s1s[t, lo + k] = term[lax.rem(lo + k, slots), ds(opp(p) * sec, sec), c].astype(bf16)
            start(far(lo, n, t), S_FAR, FAR + lo)
            for k in range(n):
                b = lo + k
                slot = lax.rem(b, slots)
                s2s[t, 0, b, pl.ds(h, h)] = term[slot, ds(up1(p) * sec + h, h), c].astype(bf16)
                s2s[t, 1, b, pl.ds(0, h)] = term[slot, ds(dn1(p) * sec, h), c].astype(bf16)
            if split:
                start(near_part(lo, t, True), S_NEAR, OWN + lo)

    def reduce1(lo, n, split):
        arrive(s1r.at[:, :, pl.ds(lo, n)], FAR + lo)
        for t in range(2):
            p, _ = pos[t]
            c = pl.ds(t * half, half)
            for k in range(n):
                b = lo + k
                slot = lax.rem(b, slots)
                s2s[t, 0, b, pl.ds(0, h)] = (
                    term[slot, ds(up1(p) * sec, h), c] + s1r[t, 0, b].astype(f32)).astype(bf16)
                s2s[t, 1, b, pl.ds(h, h)] = (
                    term[slot, ds(dn1(p) * sec + h, h), c] + s1r[t, 1, b].astype(f32)).astype(bf16)
            start(near_part(lo, t, False) if split else near(lo, n, t), S_NEAR, NEAR + lo)
        for t in range(2):
            p, _ = pos[t]
            for k in range(n):
                own[t, lo + k] = term[
                    lax.rem(lo + k, slots), ds(p * sec, sec), pl.ds(t * half, half)]

    def reduce2(g, lo, n):
        for b in range(lo, lo + n):
            if b < SPLIT:
                arrive(s1r.at[:, :, b], OWN + b)
                arrive(s1r.at[:, :, b], NEAR + b)
            else:
                arrive(s2r.at[:, :, b], NEAR + b)
        for t in range(2):
            _, q = pos[t]
            for b in range(lo, lo + n):
                own[t, b] = own[t, b] + s2r[t, 0, b].astype(f32) + s2r[t, 1, b].astype(f32)
                s3s[t, b] = own[t, b, ds(opp(q) * piece, piece), :].astype(bf16)
            start(far2(lo, n, t), S_FAR2, FAR2 + g)

    def reduce3(g, lo, n):
        left, right = pl.ds(0, quarter), pl.ds(quarter, quarter)
        arrive(s3r.at[:, :, pl.ds(lo, n)], FAR2 + g)
        for t in range(2):
            _, q = pos[t]
            r, l = ds(up1(q) * piece, piece), ds(dn1(q) * piece, piece)
            for b in range(lo, lo + n):
                s4s[t, 0, b, :, left] = (
                    own[t, b, r, left] + s3r[t, 0, b].astype(f32)).astype(bf16)
                s4s[t, 0, b, :, right] = own[t, b, r, right].astype(bf16)
                s4s[t, 1, b, :, left] = own[t, b, l, left].astype(bf16)
                s4s[t, 1, b, :, right] = (
                    own[t, b, l, right] + s3r[t, 1, b].astype(f32)).astype(bf16)
            start(near2(lo, n, t), S_NEAR2, NEAR2 + g)

    def g1_sem(g, lo):
        return FAR + lo + 1 if g < GROUPS - 1 else LAST

    def reduce4(g, lo, n):
        arrive(s4r.at[:, :, pl.ds(lo, n)], NEAR2 + g)
        for t in range(2):
            p, q = pos[t]
            for b in range(lo, lo + n):
                y[b, ds(p * sec + q * piece, piece), pl.ds(t * half, half)] = (
                    own[t, b, ds(q * piece, piece), :]
                    + s4r[t, 0, b].astype(f32) + s4r[t, 1, b].astype(f32)).astype(bf16)
            start(gather1(lo, n, t), S_NEAR2, g1_sem(g, lo))

    def send2(g, lo, n):
        arrive(s4r.at[:, :, pl.ds(lo, n)], g1_sem(g, lo))
        for t in range(2):
            start(gather2(lo, n, t), S_FAR2, FAR2 + g)

    def got2(g, lo, n):
        arrive(s3r.at[:, :, pl.ds(lo, n)], FAR2 + g)

    def send3(lo, n):
        for t in range(2):
            start(gather3(lo, n, t), S_NEAR, FAR + lo)

    def send4(lo, n):
        arrive(s2r.at[:, :, pl.ds(lo, n)], FAR + lo)
        for t in range(2):
            start(gather4(lo, n, t), S_FAR, NEAR + lo)

    def got4(lo, n):
        arrive(s1r.at[:, :, pl.ds(lo, n)], NEAR + lo)

    x_copy(0).wait()
    for n in range(3):
        for c in load_in(n):
            c.wait()
        if n == 1:
            for k in range(d // OUT0):
                load_out(k).start()
            x_copy(1).start()
        hidden(0, *pieces0[n])
    for t in range(2):
        for n in range(t * half // OUT0, (t + 1) * half // OUT0):
            load_out(n).wait()
            down(0, n, OUT0)
        if t == 0:
            pl.semaphore_wait(barrier, 4)
        pack(0, 1, True, (t,))
    x_copy(2).start()

    compute1(1)
    reduce1(0, 1, True)
    compute2(1)
    pack(1, 1, True)

    pair = [(g, 2 * g, 2) for g in range(GROUPS)]
    beside = {
        5: [(reduce2, *pair[0])],
        6: [(reduce2, *pair[1]), (reduce3, *pair[0])],
        7: [(reduce3, *pair[1]), (reduce4, *pair[0])],
    }

    def step(b, _):
        compute(b)

        @pl.when(b < SPLIT)
        def _():
            pack(b, 1, True)

        @pl.when(b >= SPLIT)
        def _():
            pack(b, 1, False)

        @pl.when(b <= SPLIT)
        def _():
            reduce1(b - 1, 1, True)

        @pl.when(b > SPLIT)
        def _():
            reduce1(b - 1, 1, False)

        for k, tasks in beside.items():
            @pl.when(b == k)
            def _():
                for task, *args in tasks:
                    task(*args)
        return 0

    lax.fori_loop(2, blocks, step, 0)

    for task, *args in [
        (reduce1, blocks - 1, 1, SPLIT == blocks),
        (reduce2, *pair[2]), (reduce4, *pair[1]), (send2, *pair[0]),
        (reduce3, *pair[2]), (reduce2, *pair[3]), (send2, *pair[1]),
        (got2, *pair[0]), (send3, 0, 2),
        (reduce4, *pair[2]), (reduce3, *pair[3]),
        (got2, *pair[1]), (send3, 2, 2),
        (send2, *pair[2]), (reduce4, *pair[3]),
        (got2, *pair[2]), (send3, 4, 2),
        (send2, *pair[3]), (send4, 0, 2),
        (got2, *pair[3]), (send3, 6, 1), (send3, 7, 1),
        (send4, 2, 2), (send4, 4, 2), (send4, 6, 1), (send4, 7, 1),
        (got4, 0, 2), (got4, 2, 2), (got4, 4, 2), (got4, 6, 1), (got4, 7, 1),
    ]:
        task(*args)

    for sent, like in enumerate((s2s, y, s4s, s1s)):
        pltpu.make_async_copy(like, like, send_sem.at[sent]).wait()


def solution(mesh):
    side = math.isqrt(mesh.shape["tp"])

    def step(x, w_gate, w_up, w_down):
        rows, d = x.shape
        f = w_gate.shape[1]
        blocks, sec = rows // BLOCK, BLOCK // side
        piece, half = sec // side, d // 2
        bf16, f32 = jnp.bfloat16, jnp.float32
        return pl.pallas_call(
            functools.partial(kernel, side),
            out_shape=pltpu.VMEM((blocks, BLOCK, d), bf16),
            in_specs=[pl.BlockSpec(memory_space=pl.ANY)] * 4,
            out_specs=pl.BlockSpec(memory_space=pltpu.VMEM),
            scratch_shapes=[
                pltpu.VMEM((2, BLOCK, d), bf16),
                pltpu.VMEM((d, f), bf16),
                pltpu.VMEM((d, f), bf16),
                pltpu.VMEM((f, d), bf16),
                pltpu.VMEM((BLOCK, f), bf16),
                pltpu.VMEM((4, BLOCK, d), f32),
                pltpu.VMEM((2, blocks, sec, half), f32),
                pltpu.VMEM((2, blocks, sec, half), bf16),
                pltpu.VMEM((2, 2, blocks, sec // 2, half), bf16),
                pltpu.VMEM((2, 2, blocks, sec, half), bf16),
                pltpu.VMEM((2, 2, blocks, sec, half), bf16),
                pltpu.VMEM((2, blocks, piece, half), bf16),
                pltpu.VMEM((2, 2, blocks, piece, half // 2), bf16),
                pltpu.VMEM((2, 2, blocks, piece, half), bf16),
                pltpu.VMEM((2, 2, blocks, piece, half), bf16),
                pltpu.SemaphoreType.DMA((2,)),
                pltpu.SemaphoreType.DMA((3,)),
                pltpu.SemaphoreType.DMA((3,)),
                pltpu.SemaphoreType.DMA((d // OUT0,)),
                pltpu.SemaphoreType.DMA((4,)),
                pltpu.SemaphoreType.DMA((2 * blocks + 2 * GROUPS + SPLIT + 1,)),
            ],
            compiler_params=pltpu.CompilerParams(
                collective_id=0, has_side_effects=True, vmem_limit_bytes=50 * 2**20),
        )(x, w_gate, w_up, w_down).reshape(rows, d)

    return jax.shard_map(
        step,
        mesh=mesh,
        in_specs=(P("dp", None), P(None, "tp"), P(None, "tp"), P("tp", None)),
        out_specs=P("dp", None),
        check_vma=False,
    )
```

time: 105 us -> 103 us (0.981)
  Pallas kernels: 101 us -> 99.2 us
    pallas_call x1, Pallas kernels: 101 us -> 99.2 us  [step(): pl.pallas_call(functools.partial(kernel, side), out_shape=pltpu.VMEM((blo...]
where the time goes in v3:
time: 103 us
  Pallas kernels  99.2 us (96%)
  local copies, waits for them, and re-layouts  3.4 us (3%)
    pallas_call x1, Pallas kernels, step(): pl.pallas_call(functools.partial(kernel, side), out_shape=pltpu.VMEM((blo...  99.2 us
    unnamed x1, local copies, waits for them, and re-layouts  3.4 us

profile of v3, /device:TPU:96, one launch (start us, length us, event | category | flops | bytes accessed | tf_op | source)
XLA Modules:
  0.0 102.7 jit_solution(1309381776586430063)
XLA Ops:
  0.0 99.2 %shard_map.46 = bf16[8,256,2048]{2,1,0:T(8,128)(2,1)S(1)} custom-call(bf16[2048,2048]{1,0:T(8,128)(2,1)} %x_hbm.1, bf16[2048,1024]{1,0:T(8,128)(2,1)} %wg_hbm.1, bf16[2048,1024]{1,0:T(8,128)(2,1)} %wu_hbm.1, bf16[1024,2048]{1,0:T(8,128)(2,1)} %wd_hbm.1), custom_call_target="tpu_custom_call" | custom-call | tf_op jit(solution)/shard_map/pallas_call | solution.py:346
  99.2 3.4 %copy.6 = bf16[2048,2048]{1,0:T(8,128)(2,1)} copy(bf16[2048,2048]{1,0:T(8,128)(2,1)S(1)} %bitcast.1) | data formatting | bytes 16777216

commit v4 on v3

--- a/solution.py
+++ b/solution.py
@@ -13,7 +13,6 @@
 HID0, OUT0 = 256, 1024
 HID, OUT = 512, 1024
 GROUPS = 4
-SPLIT = 5
 
 
 def kernel(side, x_hbm, wg_hbm, wu_hbm, wd_hbm, y, xb, wg, wu, wd, hid, term, own,
@@ -91,27 +90,20 @@
         for n in range(f // HID):
             hidden(lax.rem(b, 2), n * HID, HID)
 
-    def compute2(b):
-        for n in range(d // OUT):
+    def compute2(b, t):
+        for n in range(t * half // OUT, (t + 1) * half // OUT):
             down(lax.rem(b, slots), n, OUT)
-
+        pack(b, t)
+
+    def next_rows(b):
         @pl.when(b + 2 < blocks)
         def _():
             x_copy(b + 2).start()
 
-    def compute(b):
-        compute1(b)
-        compute2(b)
-
-    def far(lo, n, t):
-        bs = pl.ds(lo, n)
-        return [(s1s.at[t, bs, pl.ds(w * h, h)], s1r.at[t, w, bs], first[t][w]) for w in range(2)]
-
-    def near(lo, n, t):
-        bs = pl.ds(lo, n)
-        return [(s2s.at[t, w, bs], s2r.at[t, w, bs], first[t][w]) for w in range(2)]
-
-    def near_part(b, t, own_half):
+    def far(b, t):
+        return [(s1s.at[t, b, pl.ds(w * h, h)], s1r.at[t, w, b], first[t][w]) for w in range(2)]
+
+    def near(b, t, own_half):
         k = [pl.ds((1 - w if own_half else w) * h, h) for w in range(2)]
         return [(s2s.at[t, w, b, k[w]], s2r.at[t, w, b, k[w]], first[t][w]) for w in range(2)]
 
@@ -148,7 +140,7 @@
 
     FAR, NEAR, FAR2, NEAR2 = 0, blocks, 2 * blocks, 2 * blocks + GROUPS
     OWN = NEAR2 + GROUPS
-    LAST = OWN + SPLIT
+    LAST = OWN + blocks
     S_FAR, S_NEAR, S_FAR2, S_NEAR2 = range(4)
 
     def start(copies, sent, sem):
@@ -160,47 +152,35 @@
     def arrive(like, sem):
         pltpu.make_async_copy(like, like, recv_sem.at[sem]).wait()
 
-    def pack(lo, n, split, streams=range(2)):
-        for t in streams:
+    def pack(b, t):
+        slot = lax.rem(b, slots)
+        p, _ = pos[t]
+        c = pl.ds(t * half, half)
+        s1s[t, b] = term[slot, ds(opp(p) * sec, sec), c].astype(bf16)
+        start(far(b, t), S_FAR, FAR + b)
+        s2s[t, 0, b, pl.ds(h, h)] = term[slot, ds(up1(p) * sec + h, h), c].astype(bf16)
+        s2s[t, 1, b, pl.ds(0, h)] = term[slot, ds(dn1(p) * sec, h), c].astype(bf16)
+        start(near(b, t, True), S_NEAR, OWN + b)
+
+    def reduce1(b):
+        slot = lax.rem(b, slots)
+        arrive(s1r.at[:, :, b], FAR + b)
+        for t in range(2):
             p, _ = pos[t]
             c = pl.ds(t * half, half)
-            for k in range(n):
-                s1s[t, lo + k] = term[lax.rem(lo + k, slots), ds(opp(p) * sec, sec), c].astype(bf16)
-            start(far(lo, n, t), S_FAR, FAR + lo)
-            for k in range(n):
-                b = lo + k
-                slot = lax.rem(b, slots)
-                s2s[t, 0, b, pl.ds(h, h)] = term[slot, ds(up1(p) * sec + h, h), c].astype(bf16)
-                s2s[t, 1, b, pl.ds(0, h)] = term[slot, ds(dn1(p) * sec, h), c].astype(bf16)
-            if split:
-                start(near_part(lo, t, True), S_NEAR, OWN + lo)
-
-    def reduce1(lo, n, split):
-        arrive(s1r.at[:, :, pl.ds(lo, n)], FAR + lo)
+            s2s[t, 0, b, pl.ds(0, h)] = (
+                term[slot, ds(up1(p) * sec, h), c] + s1r[t, 0, b].astype(f32)).astype(bf16)
+            s2s[t, 1, b, pl.ds(h, h)] = (
+                term[slot, ds(dn1(p) * sec + h, h), c] + s1r[t, 1, b].astype(f32)).astype(bf16)
+            start(near(b, t, False), S_NEAR, NEAR + b)
         for t in range(2):
             p, _ = pos[t]
-            c = pl.ds(t * half, half)
-            for k in range(n):
-                b = lo + k
-                slot = lax.rem(b, slots)
-                s2s[t, 0, b, pl.ds(0, h)] = (
-                    term[slot, ds(up1(p) * sec, h), c] + s1r[t, 0, b].astype(f32)).astype(bf16)
-                s2s[t, 1, b, pl.ds(h, h)] = (
-                    term[slot, ds(dn1(p) * sec + h, h), c] + s1r[t, 1, b].astype(f32)).astype(bf16)
-            start(near_part(lo, t, False) if split else near(lo, n, t), S_NEAR, NEAR + lo)
-        for t in range(2):
-            p, _ = pos[t]
-            for k in range(n):
-                own[t, lo + k] = term[
-                    lax.rem(lo + k, slots), ds(p * sec, sec), pl.ds(t * half, half)]
+            own[t, b] = term[slot, ds(p * sec, sec), pl.ds(t * half, half)]
 
     def reduce2(g, lo, n):
         for b in range(lo, lo + n):
-            if b < SPLIT:
-                arrive(s1r.at[:, :, b], OWN + b)
-                arrive(s1r.at[:, :, b], NEAR + b)
-            else:
-                arrive(s2r.at[:, :, b], NEAR + b)
+            arrive(s1r.at[:, :, b], OWN + b)
+            arrive(s1r.at[:, :, b], NEAR + b)
         for t in range(2):
             _, q = pos[t]
             for b in range(lo, lo + n):
@@ -271,13 +251,14 @@
             down(0, n, OUT0)
         if t == 0:
             pl.semaphore_wait(barrier, 4)
-        pack(0, 1, True, (t,))
+        pack(0, t)
     x_copy(2).start()
 
     compute1(1)
-    reduce1(0, 1, True)
-    compute2(1)
-    pack(1, 1, True)
+    compute2(1, 0)
+    reduce1(0)
+    compute2(1, 1)
+    next_rows(1)
 
     pair = [(g, 2 * g, 2) for g in range(GROUPS)]
     beside = {
@@ -287,23 +268,11 @@
     }
 
     def step(b, _):
-        compute(b)
-
-        @pl.when(b < SPLIT)
-        def _():
-            pack(b, 1, True)
-
-        @pl.when(b >= SPLIT)
-        def _():
-            pack(b, 1, False)
-
-        @pl.when(b <= SPLIT)
-        def _():
-            reduce1(b - 1, 1, True)
-
-        @pl.when(b > SPLIT)
-        def _():
-            reduce1(b - 1, 1, False)
+        compute1(b)
+        compute2(b, 0)
+        compute2(b, 1)
+        next_rows(b)
+        reduce1(b - 1)
 
         for k, tasks in beside.items():
             @pl.when(b == k)
@@ -315,7 +284,7 @@
     lax.fori_loop(2, blocks, step, 0)
 
     for task, *args in [
-        (reduce1, blocks - 1, 1, SPLIT == blocks),
+        (reduce1, blocks - 1),
         (reduce2, *pair[2]), (reduce4, *pair[1]), (send2, *pair[0]),
         (reduce3, *pair[2]), (reduce2, *pair[3]), (send2, *pair[1]),
         (got2, *pair[0]), (send3, 0, 2),
@@ -369,7 +338,7 @@
                 pltpu.SemaphoreType.DMA((3,)),
                 pltpu.SemaphoreType.DMA((d // OUT0,)),
                 pltpu.SemaphoreType.DMA((4,)),
-                pltpu.SemaphoreType.DMA((2 * blocks + 2 * GROUPS + SPLIT + 1,)),
+                pltpu.SemaphoreType.DMA((3 * blocks + 2 * GROUPS + 1,)),
             ],
             compiler_params=pltpu.CompilerParams(
                 collective_id=0, has_side_effects=True, vmem_limit_bytes=50 * 2**20),

time: 103 us -> 102 us (level)
  no operation moved by 1% of the time
where the time goes in v4:
time: 102 us
  Pallas kernels  98.6 us (97%)
  local copies, waits for them, and re-layouts  3.4 us (3%)
    pallas_call x1, Pallas kernels, step(): pl.pallas_call(functools.partial(kernel, side), out_shape=pltpu.VMEM((blo...  98.6 us
    unnamed x1, local copies, waits for them, and re-layouts  3.4 us

profile of v4, /device:TPU:96, one launch (start us, length us, event | category | flops | bytes accessed | tf_op | source)
XLA Modules:
  0.0 102.0 jit_solution(17812580447659831143)
XLA Ops:
  0.0 98.6 %shard_map.46 = bf16[8,256,2048]{2,1,0:T(8,128)(2,1)S(1)} custom-call(bf16[2048,2048]{1,0:T(8,128)(2,1)} %x_hbm.1, bf16[2048,1024]{1,0:T(8,128)(2,1)} %wg_hbm.1, bf16[2048,1024]{1,0:T(8,128)(2,1)} %wu_hbm.1, bf16[1024,2048]{1,0:T(8,128)(2,1)} %wd_hbm.1), custom_call_target="tpu_custom_call" | custom-call | tf_op jit(solution)/shard_map/pallas_call | solution.py:315
  98.6 3.4 %copy.6 = bf16[2048,2048]{1,0:T(8,128)(2,1)} copy(bf16[2048,2048]{1,0:T(8,128)(2,1)S(1)} %bitcast.1) | data formatting | bytes 16777216

commit v5 on v4

--- a/solution.py
+++ b/solution.py
@@ -12,7 +12,6 @@
 BLOCK = 256
 HID0, OUT0 = 256, 1024
 HID, OUT = 512, 1024
-GROUPS = 4
 
 
 def kernel(side, x_hbm, wg_hbm, wu_hbm, wd_hbm, y, xb, wg, wu, wd, hid, term, own,
@@ -138,9 +137,7 @@
               for w, v in enumerate((dn1(p), up1(p)))]
         return [(at[w], at[w], first[t][w]) for w in range(2)]
 
-    FAR, NEAR, FAR2, NEAR2 = 0, blocks, 2 * blocks, 2 * blocks + GROUPS
-    OWN = NEAR2 + GROUPS
-    LAST = OWN + blocks
+    FAR, NEAR = 0, blocks
     S_FAR, S_NEAR, S_FAR2, S_NEAR2 = range(4)
 
     def start(copies, sent, sem):
@@ -160,7 +157,7 @@
         start(far(b, t), S_FAR, FAR + b)
         s2s[t, 0, b, pl.ds(h, h)] = term[slot, ds(up1(p) * sec + h, h), c].astype(bf16)
         s2s[t, 1, b, pl.ds(0, h)] = term[slot, ds(dn1(p) * sec, h), c].astype(bf16)
-        start(near(b, t, True), S_NEAR, OWN + b)
+        start(near(b, t, True), S_NEAR, NEAR + b)
 
     def reduce1(b):
         slot = lax.rem(b, slots)
@@ -177,20 +174,19 @@
             p, _ = pos[t]
             own[t, b] = term[slot, ds(p * sec, sec), pl.ds(t * half, half)]
 
-    def reduce2(g, lo, n):
+    def reduce2(lo, n):
         for b in range(lo, lo + n):
-            arrive(s1r.at[:, :, b], OWN + b)
-            arrive(s1r.at[:, :, b], NEAR + b)
+            arrive(s2r.at[:, :, b], NEAR + b)
         for t in range(2):
             _, q = pos[t]
             for b in range(lo, lo + n):
                 own[t, b] = own[t, b] + s2r[t, 0, b].astype(f32) + s2r[t, 1, b].astype(f32)
                 s3s[t, b] = own[t, b, ds(opp(q) * piece, piece), :].astype(bf16)
-            start(far2(lo, n, t), S_FAR2, FAR2 + g)
-
-    def reduce3(g, lo, n):
+            start(far2(lo, n, t), S_FAR2, FAR + lo + 1)
+
+    def reduce3(lo, n):
         left, right = pl.ds(0, quarter), pl.ds(quarter, quarter)
-        arrive(s3r.at[:, :, pl.ds(lo, n)], FAR2 + g)
+        arrive(s3r.at[:, :, pl.ds(lo, n)], FAR + lo + 1)
         for t in range(2):
             _, q = pos[t]
             r, l = ds(up1(q) * piece, piece), ds(dn1(q) * piece, piece)
@@ -201,28 +197,25 @@
                 s4s[t, 1, b, :, left] = own[t, b, l, left].astype(bf16)
                 s4s[t, 1, b, :, right] = (
                     own[t, b, l, right] + s3r[t, 1, b].astype(f32)).astype(bf16)
-            start(near2(lo, n, t), S_NEAR2, NEAR2 + g)
-
-    def g1_sem(g, lo):
-        return FAR + lo + 1 if g < GROUPS - 1 else LAST
-
-    def reduce4(g, lo, n):
-        arrive(s4r.at[:, :, pl.ds(lo, n)], NEAR2 + g)
+            start(near2(lo, n, t), S_NEAR2, NEAR + lo + 1)
+
+    def reduce4(lo, n):
+        arrive(s4r.at[:, :, pl.ds(lo, n)], NEAR + lo + 1)
         for t in range(2):
             p, q = pos[t]
             for b in range(lo, lo + n):
                 y[b, ds(p * sec + q * piece, piece), pl.ds(t * half, half)] = (
                     own[t, b, ds(q * piece, piece), :]
                     + s4r[t, 0, b].astype(f32) + s4r[t, 1, b].astype(f32)).astype(bf16)
-            start(gather1(lo, n, t), S_NEAR2, g1_sem(g, lo))
-
-    def send2(g, lo, n):
-        arrive(s4r.at[:, :, pl.ds(lo, n)], g1_sem(g, lo))
-        for t in range(2):
-            start(gather2(lo, n, t), S_FAR2, FAR2 + g)
-
-    def got2(g, lo, n):
-        arrive(s3r.at[:, :, pl.ds(lo, n)], FAR2 + g)
+            start(gather1(lo, n, t), S_NEAR2, FAR + lo + 1)
+
+    def send2(lo, n):
+        arrive(s4r.at[:, :, pl.ds(lo, n)], FAR + lo + 1)
+        for t in range(2):
+            start(gather2(lo, n, t), S_FAR2, NEAR + lo + 1)
+
+    def got2(lo, n):
+        arrive(s3r.at[:, :, pl.ds(lo, n)], NEAR + lo + 1)
 
     def send3(lo, n):
         for t in range(2):
@@ -260,7 +253,7 @@
     compute2(1, 1)
     next_rows(1)
 
-    pair = [(g, 2 * g, 2) for g in range(GROUPS)]
+    pair = [(b, 2) for b in range(0, blocks, 2)]
     beside = {
         5: [(reduce2, *pair[0])],
         6: [(reduce2, *pair[1]), (reduce3, *pair[0])],
@@ -338,7 +331,7 @@
                 pltpu.SemaphoreType.DMA((3,)),
                 pltpu.SemaphoreType.DMA((d // OUT0,)),
                 pltpu.SemaphoreType.DMA((4,)),
-                pltpu.SemaphoreType.DMA((3 * blocks + 2 * GROUPS + 1,)),
+                pltpu.SemaphoreType.DMA((2 * blocks,)),
             ],
             compiler_params=pltpu.CompilerParams(
                 collective_id=0, has_side_effects=True, vmem_limit_bytes=50 * 2**20),

time: 102 us -> 102 us (level)
  no operation moved by 1% of the time
where the time goes in v5:
time: 102 us
  Pallas kernels  98.4 us (96%)
  local copies, waits for them, and re-layouts  3.4 us (3%)
    pallas_call x1, Pallas kernels, step(): pl.pallas_call(functools.partial(kernel, side), out_shape=pltpu.VMEM((blo...  98.4 us
    unnamed x1, local copies, waits for them, and re-layouts  3.4 us

profile of v5, /device:TPU:96, one launch (start us, length us, event | category | flops | bytes accessed | tf_op | source)
XLA Modules:
  0.0 101.8 jit_solution(11454834755667093547)
XLA Ops:
  0.0 98.4 %shard_map.46 = bf16[8,256,2048]{2,1,0:T(8,128)(2,1)S(1)} custom-call(bf16[2048,2048]{1,0:T(8,128)(2,1)} %x_hbm.1, bf16[2048,1024]{1,0:T(8,128)(2,1)} %wg_hbm.1, bf16[2048,1024]{1,0:T(8,128)(2,1)} %wu_hbm.1, bf16[1024,2048]{1,0:T(8,128)(2,1)} %wd_hbm.1), custom_call_target="tpu_custom_call" | custom-call | tf_op jit(solution)/shard_map/pallas_call | solution.py:308
  98.4 3.4 %copy.6 = bf16[2048,2048]{1,0:T(8,128)(2,1)} copy(bf16[2048,2048]{1,0:T(8,128)(2,1)S(1)} %bitcast.1) | data formatting | bytes 16777216

commit v6 on v5

--- a/solution.py
+++ b/solution.py
@@ -11,7 +11,7 @@
 MESH = pl.DeviceIdType.MESH
 BLOCK = 256
 HID0, OUT0 = 256, 1024
-HID, OUT = 512, 1024
+HID, OUT = 1024, 1024
 
 
 def kernel(side, x_hbm, wg_hbm, wu_hbm, wd_hbm, y, xb, wg, wu, wd, hid, term, own,
@@ -233,7 +233,7 @@
     for n in range(3):
         for c in load_in(n):
             c.wait()
-        if n == 1:
+        if n == 0:
             for k in range(d // OUT0):
                 load_out(k).start()
             x_copy(1).start()

time: 102 us -> 102 us (level)
  no operation moved by 1% of the time
where the time goes in v6:
time: 102 us
  Pallas kernels  98.4 us (96%)
  local copies, waits for them, and re-layouts  3.4 us (3%)
    pallas_call x1, Pallas kernels, step(): pl.pallas_call(functools.partial(kernel, side), out_shape=pltpu.VMEM((blo...  98.4 us
    unnamed x1, local copies, waits for them, and re-layouts  3.4 us

profile of v6, /device:TPU:96, one launch (start us, length us, event | category | flops | bytes accessed | tf_op | source)
XLA Modules:
  0.0 101.8 jit_solution(8009218694593265734)
XLA Ops:
  0.0 98.4 %shard_map.46 = bf16[8,256,2048]{2,1,0:T(8,128)(2,1)S(1)} custom-call(bf16[2048,2048]{1,0:T(8,128)(2,1)} %x_hbm.1, bf16[2048,1024]{1,0:T(8,128)(2,1)} %wg_hbm.1, bf16[2048,1024]{1,0:T(8,128)(2,1)} %wu_hbm.1, bf16[1024,2048]{1,0:T(8,128)(2,1)} %wd_hbm.1), custom_call_target="tpu_custom_call" | custom-call | tf_op jit(solution)/shard_map/pallas_call | solution.py:308
  98.4 3.4 %copy.6 = bf16[2048,2048]{1,0:T(8,128)(2,1)} copy(bf16[2048,2048]{1,0:T(8,128)(2,1)S(1)} %bitcast.1) | data formatting | bytes 16777216

commit v7 on v6

--- a/solution.py
+++ b/solution.py
@@ -137,7 +137,7 @@
               for w, v in enumerate((dn1(p), up1(p)))]
         return [(at[w], at[w], first[t][w]) for w in range(2)]
 
-    FAR, NEAR = 0, blocks
+    FAR, NEAR, AHEAD = 0, blocks, 2 * blocks
     S_FAR, S_NEAR, S_FAR2, S_NEAR2 = range(4)
 
     def start(copies, sent, sem):
@@ -154,15 +154,15 @@
         p, _ = pos[t]
         c = pl.ds(t * half, half)
         s1s[t, b] = term[slot, ds(opp(p) * sec, sec), c].astype(bf16)
-        start(far(b, t), S_FAR, FAR + b)
+        start(far(b, t), S_FAR, (FAR, AHEAD)[t] + b)
         s2s[t, 0, b, pl.ds(h, h)] = term[slot, ds(up1(p) * sec + h, h), c].astype(bf16)
         s2s[t, 1, b, pl.ds(0, h)] = term[slot, ds(dn1(p) * sec, h), c].astype(bf16)
         start(near(b, t, True), S_NEAR, NEAR + b)
 
     def reduce1(b):
         slot = lax.rem(b, slots)
-        arrive(s1r.at[:, :, b], FAR + b)
-        for t in range(2):
+        for t in range(2):
+            arrive(s1r.at[t, :, b], (FAR, AHEAD)[t] + b)
             p, _ = pos[t]
             c = pl.ds(t * half, half)
             s2s[t, 0, b, pl.ds(0, h)] = (
@@ -331,7 +331,7 @@
                 pltpu.SemaphoreType.DMA((3,)),
                 pltpu.SemaphoreType.DMA((d // OUT0,)),
                 pltpu.SemaphoreType.DMA((4,)),
-                pltpu.SemaphoreType.DMA((2 * blocks,)),
+                pltpu.SemaphoreType.DMA((3 * blocks,)),
             ],
             compiler_params=pltpu.CompilerParams(
                 collective_id=0, has_side_effects=True, vmem_limit_bytes=50 * 2**20),

time: 102 us -> 102 us (level)
  no operation moved by 1% of the time
where the time goes in v7:
time: 102 us
  Pallas kernels  98.4 us (96%)
  local copies, waits for them, and re-layouts  3.4 us (3%)
    pallas_call x1, Pallas kernels, step(): pl.pallas_call(functools.partial(kernel, side), out_shape=pltpu.VMEM((blo...  98.4 us
    unnamed x1, local copies, waits for them, and re-layouts  3.4 us

profile of v7, /device:TPU:96, one launch (start us, length us, event | category | flops | bytes accessed | tf_op | source)
XLA Modules:
  0.0 101.8 jit_solution(977525679322018293)
XLA Ops:
  0.0 98.4 %shard_map.46 = bf16[8,256,2048]{2,1,0:T(8,128)(2,1)S(1)} custom-call(bf16[2048,2048]{1,0:T(8,128)(2,1)} %x_hbm.1, bf16[2048,1024]{1,0:T(8,128)(2,1)} %wg_hbm.1, bf16[2048,1024]{1,0:T(8,128)(2,1)} %wu_hbm.1, bf16[1024,2048]{1,0:T(8,128)(2,1)} %wd_hbm.1), custom_call_target="tpu_custom_call" | custom-call | tf_op jit(solution)/shard_map/pallas_call | solution.py:308
  98.4 3.4 %copy.6 = bf16[2048,2048]{1,0:T(8,128)(2,1)} copy(bf16[2048,2048]{1,0:T(8,128)(2,1)S(1)} %bitcast.1) | data formatting | bytes 16777216
